TPU v7x, 128 devices: a whole 4x4x4 slice. The times are simulated.
128 devices in a mesh: seq: 16 (over x_hi, z, core), tp: 8 (over y, x_lo).
Axes of the slice: x: 4 (x_hi: 2, x_lo: 2; x = x_hi * 2 + x_lo), y: 4, z: 4, core: 2. Of those that a mesh axis runs over, the one named last changes fastest.
Arguments:
- tokens: bfloat16 [2048, 8192], P('seq'), may hold values from -6 to 6
- conv_weight: float32 [4, 8192], replicated, may hold values from -3 to 3
- norm_gain: float32 [8192], replicated, may hold values from 0.25 to 1.75
- gate_weight: bfloat16 [8192, 14336], P('seq', 'tp'), may hold values from -0.0625 to 0.0625
- up_weight: bfloat16 [8192, 14336], P('seq', 'tp'), may hold values from -0.0625 to 0.0625
- down_weight: bfloat16 [14336, 8192], P('tp', 'seq'), may hold values from -0.046875 to 0.046875
Outputs:
- mixed_out: bfloat16 [2048, 8192], P(('seq', 'tp'))
All inputs are finite; a program needn't handle non-finite values.
Results may differ from a plain program's by a relative error of at most 0.03.
Values may be sent and summed in bfloat16 or wider, within the bound.
No kernel may reach another device: no remote copies, remote signals or barrier semaphores. Data moves between devices by JAX's collectives and lax.ppermute only.
A program may use at most 64 MiB of HBM per device.

v0:
```python
import jax
import jax.numpy as jnp
from jax import lax
from jax.sharding import PartitionSpec as P


def from_behind(shard, axis, by):
    peers = lax.axis_size(axis)
    pairs = [(i, i + by) for i in range(peers) if 0 <= i + by < peers]
    return lax.ppermute(shard, axis, pairs)


def split_up(shard, dim, peers):
    shape = shard.shape
    parts = shard.reshape(*shape[:dim], peers, shape[dim] // peers, *shape[dim + 1 :])
    return jnp.moveaxis(parts, dim, 0)


def summed_on_arrival(shard, axis, dim):
    parts = split_up(shard, dim, lax.axis_size(axis))
    arrived = lax.all_to_all(parts, axis, split_axis=0, concat_axis=0, tiled=True)
    return arrived.astype(jnp.float32).sum(axis=0)


def swiglu(both_sums, half_cols):
    return (jax.nn.silu(both_sums[:, :half_cols]) * both_sums[:, half_cols:]).astype(jnp.bfloat16)


def shards(tokens, conv_weight, norm_gain, gate_weight, up_weight, down_weight):
    tok_rows = tokens.shape[0]
    taps_count = conv_weight.shape[0]
    seq_count = lax.axis_size("seq")
    edge_rows = from_behind(tokens[tok_rows - (taps_count - 1) :], "seq", 1)
    extended = jnp.concatenate([edge_rows, tokens], 0).astype(jnp.float32)
    conv_out = jnp.zeros(tokens.shape, jnp.float32)
    for tap_index in range(taps_count):
        begin = taps_count - 1 - tap_index
        conv_out = conv_out + conv_weight[tap_index][None, :] * extended[begin : begin + tok_rows]
    scale_rms = lax.rsqrt(jnp.mean(conv_out * conv_out, axis=-1, keepdims=True) + 1e-05)
    normed = (conv_out * scale_rms * norm_gain[None, :]).astype(jnp.bfloat16)
    all_rows = lax.all_to_all(normed, "seq", split_axis=1, concat_axis=0, tiled=True)
    half_cols = gate_weight.shape[1]
    w_both = jnp.concatenate([gate_weight, up_weight], 1)
    gate_share = lax.psum_scatter(
        jnp.dot(all_rows, w_both, preferred_element_type=jnp.float32).astype(jnp.bfloat16),
        "seq",
        scatter_dimension=0,
        tiled=True,
    ).astype(jnp.float32)
    hidden = swiglu(gate_share, half_cols)
    out_terms = jnp.dot(
        lax.all_gather(hidden, "seq", axis=0, tiled=True),
        down_weight,
        preferred_element_type=jnp.float32,
    )
    col_width = out_terms.shape[1]
    out_terms = out_terms.reshape(seq_count, tok_rows, col_width)
    summed = summed_on_arrival(out_terms.astype(jnp.bfloat16), "tp", 1)
    rounded = summed.astype(jnp.bfloat16)
    mixed_out = lax.all_to_all(rounded, "seq", split_axis=0, concat_axis=2, tiled=True)
    return mixed_out.reshape(mixed_out.shape[1], mixed_out.shape[2])


def solution(mesh):
    in_specs = (P("seq", None), P(), P(), P("seq", "tp"), P("seq", "tp"), P("tp", "seq"))
    out_specs = P(("seq", "tp"), None)
    return jax.shard_map(shards, mesh=mesh, in_specs=in_specs, out_specs=out_specs, check_vma=False)
```

profile of v0, /device:TPU:1, one launch (start us, length us, event | category | flops | bytes accessed | tf_op | source)
XLA Modules:
  0.0 350.1 jit_solution(9454202880680602987)
XLA Ops:
  6.5 0.0 copy-start
  6.5 0.0 reduce-scatter.2.cloned.1.call-start
  6.5 1.1 slice.34
  7.6 4.9 %collective-permute-start = (bf16[3,8192]{1,0:T(4,128)(2,1)S(1)}, bf16[3,8192]{1,0:T(4,128)(2,1)S(1)}, u32[]{:S(2)}, u32[]{:S(2)}) collective-permute-start(bf16[3,8192]{1,0:T(4,128)(2,1)S(1)} %slice.34), channel_id=1, source_target_pairs={{0,8},{8,16},{16,24},{24,32},{32,40},{40,48},{48,56},{56,64},{64,7... | collective-permute-start | bytes 147464 | tf_op jit(solution)/shard_map/ppermute | solution.py:10
  12.5 1.4 fusion.9
  13.9 4.1 %copy.16 = bf16[128,8192]{0,1:T(8,128)(2,1)} copy(bf16[128,8192]{1,0:T(8,128)(2,1)} %param.6) | data formatting | bytes 4194304 | tf_op args[0]
  18.0 0.0 collective-permute-done
  18.0 1.8 copy.15
  19.8 3.7 %maximum_convert_fusion = f32[131,8192]{0,1:T(8,128)S(1)} fusion(bf16[128,8192]{0,1:T(8,128)(2,1)} %copy.16, bf16[3,8192]{0,1:T(8,128)(2,1)} %copy.15), kind=kLoop, calls=%fused_computation.8 | loop fusion | flops 4292608 | bytes 6438912 | tf_op jit(solution)/shard_map/convert_element_type | solution.py:34
  23.6 0.0 copy-start.1
  23.6 8.7 %multiply_reduce_fusion = (f32[128]{0:T(128)S(1)}, f32[128,8192]{0,1:T(8,128)S(1)}) fusion(f32[131,8192]{0,1:T(8,128)S(1)} %maximum_convert_fusion, f32[8192]{0:T(1024)S(1)} %bitcast.30, f32[8192]{0:T(1024)S(1)} %bitcast.31, f32[8192]{0:T(1024)S(1)} %bitcast.29, f32[8192]{0:T(1024)S(1)} %bitcast.28), kind=kLoop, calls=%fused_computation.10 | loop fusion | flops 9437056 | bytes 21103104 | tf_op jit(solution)/shard_map/reduce_sum | solution.py:39
  32.3 0.0 copy-done.1
  32.3 3.5 multiply_convert_fusion
  35.8 35.4 %all_to_all.39 = bf16[128,16,512]{0,2,1:T(8,128)(2,1)} all-to-all(bf16[128,16,512]{0,2,1:T(8,128)(2,1)S(1)} %bitcast.22), channel_id=1, replica_groups=mesh['seq'=16,'tp'=8] {'seq'}, dimensions={1} | all-to-all | bytes 4194304 | tf_op jit(solution)/shard_map/all_to_all | solution.py:41
  71.2 3.9 %copy.17 = bf16[16,128,512]{2,1,0:T(8,128)(2,1)} copy(bf16[16,128,512]{1,2,0:T(8,128)(2,1)} %bitcast.23) | data formatting | bytes 4194304 | tf_op jit(solution)/shard_map/all_to_all | solution.py:41
  75.1 13.4 %convolution_convert_fusion = bf16[2048,3584]{1,0:T(8,128)(2,1)} fusion(bf16[2048,512]{1,0:T(8,128)(2,1)} %bitcast.25, bf16[512,1792]{1,0:T(8,128)(2,1)} %param.10, bf16[512,1792]{1,0:T(8,128)(2,1)} %param.9), kind=kOutput, calls=%fused_computation | convolution fusion | flops 7530872832 | bytes 20447232 | tf_op jit(solution)/shard_map/dot_general | solution.py:45
  88.5 0.0 reduce-scatter.2.cloned.1.call-update
  88.5 0.0 all-gather.2.cloned.1.call-start
  88.6 129.9 %reduce-scatter.2.cloned.1.call-done = bf16[128,3584]{1,0:T(8,128)(2,1)} async-done(((bf16[2048,3584]{1,0:T(8,128)(2,1)}), bf16[128,3584]{1,0:T(8,128)(2,1)}) %reduce-scatter.2.cloned.1.call-update) | async-done | bytes 917520 | tf_op jit(solution)/shard_map/reduce_scatter | solution.py:44
  218.4 1.4 convert_element_type.27
  219.8 1.0 fusion.6
  220.8 0.0 all-gather.2.cloned.1.call-update
  220.8 67.8 %all-gather.2.cloned.1.call-done = bf16[2048,1792]{1,0:T(8,128)(2,1)} async-done(((bf16[128,1792]{1,0:T(8,128)(2,1)}), bf16[2048,1792]{1,0:T(8,128)(2,1)}) %all-gather.2.cloned.1.call-update) | async-done | bytes 7340048 | tf_op jit(solution)/shard_map/all_gather | solution.py:52
  288.6 0.0 copy-done
  288.7 7.3 %convolution_convert_fusion.1 = bf16[2048,512]{1,0:T(8,128)(2,1)S(1)} fusion(bf16[2048,1792]{1,0:T(8,128)(2,1)} %all-gather.2.cloned.1.call-done, bf16[1792,512]{1,0:T(8,128)(2,1)S(1)} %copy-done), kind=kOutput, calls=%fused_computation.14 | convolution fusion | flops 3759144960 | bytes 11272192 | tf_op jit(solution)/shard_map/dot_general | solution.py:51
  295.9 0.2 copy.25
  296.1 30.1 %all_to_all.40 = bf16[8,16,16,512]{3,2,1,0:T(8,128)(2,1)} all-to-all(bf16[8,16,16,512]{3,2,1,0:T(8,128)(2,1)S(1)} %bitcast.24), channel_id=1, replica_groups=mesh['seq'=16,'tp'=8] {'tp'}, dimensions={0} | all-to-all | bytes 4194304 | tf_op jit(solution)/shard_map/all_to_all | solution.py:21
  326.2 2.0 reduce_sum.22
  328.2 14.4 %all_to_all.41 = bf16[16,16,512]{2,1,0:T(8,128)(2,1)S(1)} all-to-all(bf16[16,16,512]{2,1,0:T(8,128)(2,1)S(1)} %reduce_sum.22), channel_id=1, replica_groups=mesh['seq'=16,'tp'=8] {'seq'}, dimensions={0} | all-to-all | bytes 524288 | tf_op jit(solution)/shard_map/all_to_all | solution.py:60
  342.6 0.7 copy.22
  (1 shorter events, 0.0 us)
Async XLA Ops:
  6.5 282.1 %copy-start = (bf16[1792,512]{1,0:T(8,128)(2,1)S(1)}, bf16[1792,512]{1,0:T(8,128)(2,1)}, u32[]{:S(2)}) copy-start(bf16[1792,512]{1,0:T(8,128)(2,1)} %param.11) | copy-start | bytes 5505028
  6.5 211.9 %reduce-scatter.2.cloned.1.call-start = ((), (), s32[]{:S(2)}) async-start(), calls=%async_computation.4 | async-start | bytes 15597568 | tf_op jit(solution)/shard_map/reduce_scatter | solution.py:44
  7.6 10.4 %collective-permute-start = (bf16[3,8192]{1,0:T(4,128)(2,1)S(1)}, bf16[3,8192]{1,0:T(4,128)(2,1)S(1)}, u32[]{:S(2)}, u32[]{:S(2)}) collective-permute-start(bf16[3,8192]{1,0:T(4,128)(2,1)S(1)} %slice.34), channel_id=1, source_target_pairs={{0,8},{8,16},{16,24},{24,32},{32,40},{40,48},{48,56},{56,64},{64,7... | collective-permute-start | bytes 147464 | tf_op jit(solution)/shard_map/ppermute | solution.py:10
  23.6 8.8 %copy-start.1 = (f32[8192]{0:T(1024)S(1)}, f32[8192]{0:T(1024)}, u32[]{:S(2)}) copy-start(f32[8192]{0:T(1024)} %param.8) | copy-start | bytes 98308
  88.5 200.1 %all-gather.2.cloned.1.call-start = ((), (), s32[]{:S(2)}) async-start(), calls=%async_computation.5 | async-start | bytes 7798784 | tf_op jit(solution)/shard_map/all_gather | solution.py:52
Sparse Core Ops, SparseCore 0:
  88.6 129.7 reduce-scatter.1
  221.0 67.6 all-gather.1
where the time goes:
time: 351 us; the launch traced here: 350 us
  waiting for transfers between devices  198 us (56%)
  blocking collectives  79.8 us (23%)
  matrix products  20.6 us (6%)
  other arithmetic  20.3 us (6%)
  between operations  13.5 us (4%)
  local copies, waits for them, and re-layouts  13.2 us (4%)
  starting transfers between devices  4.97 us (1%)
    reduce_scatter x1, waiting for transfers between devices, shards(): lax.psum_scatter(jnp.dot(all_rows, w_both, preferred_element_type=jnp.flo...  130 us
    all_gather x1, waiting for transfers between devices, shards(): lax.all_gather(hidden, 'seq', axis=0, tiled=True)  67.8 us
    all_to_all x1, blocking collectives, shards(): lax.all_to_all(normed, 'seq', split_axis=1, concat_axis=0, tiled=True)  35.4 us
    all_to_all x1, blocking collectives, summed_on_arrival(): lax.all_to_all(parts, axis, split_axis=0, concat_axis=0, tiled=True)  30.1 us
    all_to_all x1, blocking collectives, shards(): lax.all_to_all(rounded, 'seq', split_axis=0, concat_axis=2, tiled=True)  14.4 us
    dot_general x1, matrix products, shards(): jnp.dot(all_rows, w_both, preferred_element_type=jnp.float32)  13.4 us
    reduce_sum x1, other arithmetic, shards(): jnp.mean(conv_out * conv_out, axis=-1, keepdims=True) + 1e-05  8.75 us
    dot_general x1, matrix products, shards(): jnp.dot(lax.all_gather(hidden, 'seq', axis=0, tiled=True), down_weight, p...  7.26 us
  transfers between devices with their start and end apart: 3, of which 2 were waited for; matrix products, arithmetic and copies ran while one was open for 2% of the time, Pallas kernels for 0%

commit v1 on v0

--- a/solution.py
+++ b/solution.py
@@ -49,7 +49,9 @@
     ).astype(jnp.float32)
     hidden = swiglu(gate_share, half_cols)
     out_terms = jnp.dot(
-        lax.all_gather(hidden, "seq", axis=0, tiled=True),
+        jnp.concatenate(
+            lax.all_to_all(jnp.stack([hidden] * lax.axis_size("seq")), "seq", 0, 0), axis=0
+        ),
         down_weight,
         preferred_element_type=jnp.float32,
     )

time: 351 us -> 369 us (1.051)
  blocking collectives: 79.8 us -> 169 us
  waiting for transfers between devices: 198 us -> 130 us
    all_to_all x0 -> x1, blocking collectives: none -> 88.6 us  [shards(): lax.all_to_all(jnp.stack([hidden] * lax.axis_size('seq')), 'seq', 0, 0)]
    all_gather x1 -> x0, waiting for transfers between devices: 67.8 us -> none  [shards(): lax.all_gather(hidden, 'seq', axis=0, tiled=True)]
  transfers between devices with their start and end apart: 3 -> 2, of which waited for: 2 -> 1; matrix products, arithmetic and copies ran while one was open for 2% -> 1% of each run, Pallas kernels for 0% -> 0%
where the time goes in v1:
time: 369 us
  blocking collectives  169 us (46%)
  waiting for transfers between devices  130 us (35%)
  other arithmetic  19.5 us (5%)
  matrix products  17.5 us (5%)
  local copies, waits for them, and re-layouts  13.9 us (4%)
  between operations  13.5 us (4%)
  starting transfers between devices  4.93 us (1%)
    reduce_scatter x1, waiting for transfers between devices, shards(): lax.psum_scatter(jnp.dot(all_rows, w_both, preferred_element_type=jnp.flo...  130 us
    all_to_all x1, blocking collectives, shards(): lax.all_to_all(jnp.stack([hidden] * lax.axis_size('seq')), 'seq', 0, 0)  88.6 us
    all_to_all x1, blocking collectives, shards(): lax.all_to_all(normed, 'seq', split_axis=1, concat_axis=0, tiled=True)  35.4 us
    all_to_all x1, blocking collectives, summed_on_arrival(): lax.all_to_all(parts, axis, split_axis=0, concat_axis=0, tiled=True)  30.3 us
    all_to_all x1, blocking collectives, shards(): lax.all_to_all(rounded, 'seq', split_axis=0, concat_axis=2, tiled=True)  15.1 us
    dot_general x1, matrix products, shards(): jnp.dot(all_rows, w_both, preferred_element_type=jnp.float32)  13.4 us
    reduce_sum x1, other arithmetic, shards(): jnp.mean(conv_out * conv_out, axis=-1, keepdims=True) + 1e-05  8.75 us
  transfers between devices with their start and end apart: 2, of which 1 were waited for; matrix products, arithmetic and copies ran while one was open for 1% of the time, Pallas kernels for 0%

profile of v1, /device:TPU:1, one launch (start us, length us, event | category | flops | bytes accessed | tf_op | source)
XLA Modules:
  0.0 368.5 jit_solution(6847087268541967688)
XLA Ops:
  6.5 0.0 copy-start
  6.5 0.0 reduce-scatter.2.cloned.1.call-start
  6.5 1.1 slice.34
  7.6 4.9 %collective-permute-start = (bf16[3,8192]{1,0:T(4,128)(2,1)S(1)}, bf16[3,8192]{1,0:T(4,128)(2,1)S(1)}, u32[]{:S(2)}, u32[]{:S(2)}) collective-permute-start(bf16[3,8192]{1,0:T(4,128)(2,1)S(1)} %slice.34), channel_id=1, source_target_pairs={{0,8},{8,16},{16,24},{24,32},{32,40},{40,48},{48,56},{56,64},{64,7... | collective-permute-start | bytes 147464 | tf_op jit(solution)/shard_map/ppermute | solution.py:10
  12.5 1.4 fusion.10
  13.9 4.1 %copy.16 = bf16[128,8192]{0,1:T(8,128)(2,1)} copy(bf16[128,8192]{1,0:T(8,128)(2,1)} %param.6) | data formatting | bytes 4194304 | tf_op args[0]
  18.0 0.0 collective-permute-done
  18.0 1.8 copy.15
  19.9 3.7 %maximum_convert_fusion = f32[131,8192]{0,1:T(8,128)S(1)} fusion(bf16[128,8192]{0,1:T(8,128)(2,1)} %copy.16, bf16[3,8192]{0,1:T(8,128)(2,1)} %copy.15), kind=kLoop, calls=%fused_computation.8 | loop fusion | flops 4292608 | bytes 6438912 | tf_op jit(solution)/shard_map/convert_element_type | solution.py:34
  23.6 0.0 copy-start.1
  23.6 8.7 %multiply_reduce_fusion = (f32[128]{0:T(128)S(1)}, f32[128,8192]{0,1:T(8,128)S(1)}) fusion(f32[131,8192]{0,1:T(8,128)S(1)} %maximum_convert_fusion, f32[8192]{0:T(1024)S(1)} %bitcast.32, f32[8192]{0:T(1024)S(1)} %bitcast.33, f32[8192]{0:T(1024)S(1)} %bitcast.31, f32[8192]{0:T(1024)S(1)} %bitcast.30), kind=kLoop, calls=%fused_computation.10 | loop fusion | flops 9437056 | bytes 21103104 | tf_op jit(solution)/shard_map/reduce_sum | solution.py:39
  32.4 0.0 copy-done.1
  32.4 3.5 multiply_convert_fusion
  35.9 35.4 %all_to_all.44 = bf16[128,16,512]{0,2,1:T(8,128)(2,1)} all-to-all(bf16[128,16,512]{0,2,1:T(8,128)(2,1)S(1)} %bitcast.24), channel_id=1, replica_groups=mesh['seq'=16,'tp'=8] {'seq'}, dimensions={1} | all-to-all | bytes 4194304 | tf_op jit(solution)/shard_map/all_to_all | solution.py:41
  71.2 3.9 %copy.17 = bf16[16,128,512]{2,1,0:T(8,128)(2,1)} copy(bf16[16,128,512]{1,2,0:T(8,128)(2,1)} %bitcast.25) | data formatting | bytes 4194304 | tf_op jit(solution)/shard_map/all_to_all | solution.py:41
  75.1 13.4 %convolution_convert_fusion = bf16[2048,3584]{1,0:T(8,128)(2,1)} fusion(bf16[2048,512]{1,0:T(8,128)(2,1)} %bitcast.27, bf16[512,1792]{1,0:T(8,128)(2,1)} %param.10, bf16[512,1792]{1,0:T(8,128)(2,1)} %param.9), kind=kOutput, calls=%fused_computation | convolution fusion | flops 7530872832 | bytes 20447232 | tf_op jit(solution)/shard_map/dot_general | solution.py:45
  88.5 0.0 reduce-scatter.2.cloned.1.call-update
  88.5 129.9 %reduce-scatter.2.cloned.1.call-done = bf16[128,3584]{1,0:T(8,128)(2,1)} async-done(((bf16[2048,3584]{1,0:T(8,128)(2,1)}), bf16[128,3584]{1,0:T(8,128)(2,1)}) %reduce-scatter.2.cloned.1.call-update) | async-done | bytes 917520 | tf_op jit(solution)/shard_map/reduce_scatter | solution.py:44
  218.4 1.4 convert_element_type.23
  219.7 0.3 fusion.7
  220.0 0.7 stack.2
  220.7 88.6 %all_to_all.45 = bf16[16,128,1792]{2,1,0:T(8,128)(2,1)S(1)} all-to-all(bf16[16,128,1792]{2,1,0:T(8,128)(2,1)S(1)} %stack.2), channel_id=1, replica_groups=mesh['seq'=16,'tp'=8] {'seq'}, dimensions={0} | all-to-all | bytes 14680064 | tf_op jit(solution)/shard_map/all_to_all | solution.py:53
  309.3 0.0 copy-done
  309.3 4.1 %convolution_convert_fusion.1 = bf16[16,128,512]{2,1,0:T(8,128)(2,1)S(1)} fusion(bf16[16,128,1792]{2,1,0:T(8,128)(2,1)S(1)} %all_to_all.45, bf16[1792,512]{1,0:T(8,128)(2,1)S(1)} %copy-done), kind=kOutput, calls=%fused_computation.15 | convolution fusion | flops 3759144960 | bytes 11272192 | tf_op jit(solution)/shard_map/dot_general | solution.py:51
  313.4 0.2 copy.25
  313.6 30.3 %all_to_all.46 = bf16[8,16,16,512]{3,2,1,0:T(8,128)(2,1)} all-to-all(bf16[8,16,16,512]{3,2,1,0:T(8,128)(2,1)S(1)} %bitcast.26), channel_id=1, replica_groups=mesh['seq'=16,'tp'=8] {'tp'}, dimensions={0} | all-to-all | bytes 4194304 | tf_op jit(solution)/shard_map/all_to_all | solution.py:21
  343.9 2.0 reduce_sum.22
  345.9 15.1 %all_to_all.47 = bf16[16,16,512]{2,1,0:T(8,128)(2,1)S(1)} all-to-all(bf16[16,16,512]{2,1,0:T(8,128)(2,1)S(1)} %reduce_sum.22), channel_id=1, replica_groups=mesh['seq'=16,'tp'=8] {'seq'}, dimensions={0} | all-to-all | bytes 524288 | tf_op jit(solution)/shard_map/all_to_all | solution.py:62
  360.9 0.7 copy.22
  (1 shorter events, 0.0 us)
Async XLA Ops:
  6.5 302.8 %copy-start = (bf16[1792,512]{1,0:T(8,128)(2,1)S(1)}, bf16[1792,512]{1,0:T(8,128)(2,1)}, u32[]{:S(2)}) copy-start(bf16[1792,512]{1,0:T(8,128)(2,1)} %param.11) | copy-start | bytes 5505028
  6.5 211.8 %reduce-scatter.2.cloned.1.call-start = ((), (), s32[]{:S(2)}) async-start(), calls=%async_computation.5 | async-start | bytes 15597568 | tf_op jit(solution)/shard_map/reduce_scatter | solution.py:44
  7.6 10.4 %collective-permute-start = (bf16[3,8192]{1,0:T(4,128)(2,1)S(1)}, bf16[3,8192]{1,0:T(4,128)(2,1)S(1)}, u32[]{:S(2)}, u32[]{:S(2)}) collective-permute-start(bf16[3,8192]{1,0:T(4,128)(2,1)S(1)} %slice.34), channel_id=1, source_target_pairs={{0,8},{8,16},{16,24},{24,32},{32,40},{40,48},{48,56},{56,64},{64,7... | collective-permute-start | bytes 147464 | tf_op jit(solution)/shard_map/ppermute | solution.py:10
  23.6 8.8 %copy-start.1 = (f32[8192]{0:T(1024)S(1)}, f32[8192]{0:T(1024)}, u32[]{:S(2)}) copy-start(f32[8192]{0:T(1024)} %param.8) | copy-start | bytes 98308
Sparse Core Ops, SparseCore 0:
  88.6 129.6 reduce-scatter.1
